TPU v7x, 64 devices: a 2x2x8 block of a 4x4x8 slice. The times are simulated.
64 devices in a mesh: dp: 4 (over x, y), tp: 16 (over z, core).
Axes of the slice: x: 2, y: 2, z: 8, core: 2. Of those that a mesh axis runs over, the one named last changes fastest.
The devices are a block of a 4x4x8 slice.
Arguments:
- x: bfloat16 [256, 4608], P('dp'), parts along dimension 0
- k_cache: bfloat16 [256, 2048, 16, 128], P('dp', None, 'tp'), parts along dimension 0
- v_cache: bfloat16 [256, 2048, 16, 128], P('dp', None, 'tp'), parts along dimension 0
- gain_a: bfloat16 [4608], replicated
- wq: bfloat16 [4608, 4096], P(None, 'tp')
- wo: bfloat16 [4096, 4608], P('tp')
- gain_m: bfloat16 [4608], replicated
- w_gate: bfloat16 [4608, 36864], P(None, 'tp')
- w_up: bfloat16 [4608, 36864], P(None, 'tp')
- w_down: bfloat16 [36864, 4608], P('tp')
Outputs:
- output: bfloat16 [256, 4608], P('dp'), parts along dimension 0
There are 4 independent parts. A program takes and returns all parts, laid end to end along the dimension named above; an argument that names none is the same for every part.
All inputs are finite; a program needn't handle non-finite values.
Results may differ from a plain program's by a relative error of at most 0.0171.
Values are sent between devices in bfloat16 or wider.
A program may use at most 768 MiB of HBM per device.

v0:
```python
import jax
import jax.numpy as jnp
from jax import lax
from jax.sharding import PartitionSpec as P

HEAD = 128
THETA = 10000


def normed(x, gain):
    wide = x.astype(jnp.float32)
    scale = lax.rsqrt(jnp.mean(wide * wide, -1, keepdims=True) + 1e-6)
    return (wide * scale * gain.astype(jnp.float32)).astype(jnp.bfloat16)


def turned(t, place, theta):
    half = t.shape[-1] // 2
    angle = place.astype(jnp.float32)[:, None] * theta ** (-jnp.arange(half, dtype=jnp.float32) / half)
    cos, sin = jnp.cos(angle)[:, None], jnp.sin(angle)[:, None]
    a, b = t[..., :half].astype(jnp.float32), t[..., half:].astype(jnp.float32)
    return jnp.concatenate([a * cos - b * sin, b * cos + a * sin], -1).astype(jnp.bfloat16)


def matmul(a, w):
    return jnp.dot(a, w, preferred_element_type=jnp.float32).astype(jnp.bfloat16)


def einsum(form, a, b):
    return jnp.einsum(form, a.astype(jnp.float32), b.astype(jnp.float32))


def seen_by(a, wq, k_cache, v_cache, head, theta):
    batch, cache, kv_heads = k_cache.shape[:3]
    place = jnp.full((batch,), cache - 1)
    q = turned(matmul(a, wq).reshape(batch, -1, head), place, theta).reshape(batch, kv_heads, -1, head)
    scores = einsum("bgsd,bugd->bgsu", q, k_cache) * head**-0.5
    weights = jax.nn.softmax(scores, -1).astype(jnp.bfloat16)
    return einsum("bgsu,bugd->bgsd", weights, v_cache).astype(jnp.bfloat16).reshape(batch, -1)


def hidden_of(b, w_gate, w_up):
    gate = jnp.dot(b, w_gate, preferred_element_type=jnp.float32)
    up = jnp.dot(b, w_up, preferred_element_type=jnp.float32)
    return (jax.nn.silu(gate) * up).astype(jnp.bfloat16)


def solution(mesh):
    def added(t, term):
        return (t.astype(jnp.float32) + lax.psum(term.astype(jnp.bfloat16), "tp").astype(jnp.float32)).astype(jnp.bfloat16)

    def step(x, k_cache, v_cache, gain_a, wq, wo, gain_m, w_gate, w_up, w_down):
        seen = seen_by(normed(x, gain_a), wq, k_cache, v_cache, HEAD, THETA)
        h = added(x, jnp.dot(seen, wo, preferred_element_type=jnp.float32))
        return added(h, jnp.dot(hidden_of(normed(h, gain_m), w_gate, w_up), w_down, preferred_element_type=jnp.float32))

    states, cache, columns, rows_of = P("dp", None), P("dp", None, "tp", None), P(None, "tp"), P("tp", None)
    return jax.shard_map(
        step,
        mesh=mesh,
        in_specs=(states, cache, cache, P(None), columns, rows_of, P(None), columns, columns, rows_of),
        out_specs=states,
        check_vma=False,
    )
```

profile of v0, /device:TPU:21, one launch (start us, length us, event | category | flops | bytes accessed | tf_op | source)
XLA Modules:
  0.0 289.4 jit_solution(7822315800573706689)
XLA Ops:
  6.6 1.4 fusion.11
  8.1 0.7 convert_element_type.66
  8.8 2.4 convolution_convert_fusion.2
  11.2 0.1 fusion.39
  11.4 0.1 pad_maximum_fusion
  11.5 14.8 %fusion.40 = (f32[64,2]{1,0:T(8,128)S(1)}, f32[64,2,2048]{2,1,0:T(2,128)S(1)}) fusion(bf16[64,2048,1,128]{3,1,2,0:T(8,128)(2,1)} %param.11, bf16[64,2,128]{2,0,1:T(8,128)(2,1)S(1)} %pad_maximum_fusion), kind=kOutput, calls=%fused_computation.51 | convolution fusion | flops 67897344 | bytes 34636288 | tf_op jit(solution)/shard_map/sub | solution.py:37
  26.3 13.0 %fusion.19 = bf16[64,2,128]{2,1,0:T(2,128)(2,1)S(1)} fusion(bf16[64,2048,1,128]{3,1,2,0:T(8,128)(2,1)} %param.12, f32[64,2,2048]{2,1,0:T(2,128)S(1)} %get-tuple-element.12, f32[64,2]{1,0:T(8,128)S(1)} %get-tuple-element.11), kind=kOutput, calls=%fused_computation.26 | convolution fusion | flops 67649536 | bytes 34636288 | tf_op jit(solution)/shard_map/bgsu,bugd->bgsd/dot_general | solution.py:29
  39.3 0.0 copy-start.3
  39.3 0.0 copy-start.2
  39.3 0.0 copy-done
  39.3 1.4 convolution_convert_fusion.1
  40.7 0.1 all-reduce.3.cloned.1.call-update
  40.7 0.2 all-reduce.5.cloned.1.call-start
  41.0 107.7 %all-reduce.3.cloned.1.call-done = bf16[64,4608]{1,0:T(8,128)(2,1)} async-done(((bf16[64,4608]{1,0:T(8,128)(2,1)}), bf16[64,4608]{1,0:T(8,128)(2,1)}) %all-reduce.3.cloned.1.call-update) | async-done | bytes 589840 | tf_op jit(solution)/shard_map/psum | solution.py:49
  148.7 1.4 fusion.15
  150.1 0.0 slice-start
  150.1 0.0 slice-start.1
  150.1 0.0 slice-start.2
  150.1 9.2 %fusion.27 = f32[64,2304]{1,0:T(8,128)S(1)} fusion(bf16[4608,2304]{1,0:T(8,128)(2,1)} %param.17, bf16[64,4608]{1,0:T(8,128)(2,1)S(1)} %get-tuple-element.6, f32[4608]{0:T(1024)S(1)} %convert_element_type.77, f32[64]{0:T(128)S(1)} %add_rsqrt_fusion), kind=kOutput, calls=%fused_computation.32 | convolution fusion | flops 1360134144 | bytes 22432000 | tf_op jit(solution)/shard_map/dot_general | solution.py:42
  159.4 0.0 slice-start.3
  159.4 0.0 slice-start.4
  159.4 0.0 slice-start.5
  159.4 11.4 %fusion.5 = bf16[64,2304]{1,0:T(8,128)(2,1)S(1)} fusion(bf16[4608,2304]{1,0:T(8,128)(2,1)} %param.18, f32[64,2304]{1,0:T(8,128)S(1)} %fusion.27, bf16[64,4608]{1,0:T(8,128)(2,1)S(1)} %get-tuple-element.6, f32[4608]{0:T(1024)S(1)} %convert_element_type.77, f32[64]{0:T(128)S(1)} %add_rsqrt_fusion), kind=kOutput, calls=%fused_computation.8 | convolution fusion | flops 1361018880 | bytes 22726912 | tf_op jit(solution)/shard_map/dot_general | solution.py:43
  170.8 0.0 slice-done.1
  170.8 0.0 slice-done.2
  170.8 0.0 slice-done.3
  170.8 0.0 slice-done.4
  170.8 0.0 copy-start.1
  170.8 4.6 %convolution_convert_fusion = bf16[64,4608]{1,0:T(8,128)(2,1)} fusion(bf16[64,2304]{1,0:T(8,128)(2,1)S(1)} %fusion.5, bf16[2304,4608]{1,0:T(8,128)(2,1)S(1)} %bitcast.23), kind=kOutput, calls=%fused_computation.5 | convolution fusion | flops 1359249408 | bytes 22118400 | tf_op jit(solution)/shard_map/dot_general | solution.py:54
  175.4 0.1 all-reduce.5.cloned.1.call-update
  175.5 105.1 %all-reduce.5.cloned.1.call-done = bf16[64,4608]{1,0:T(8,128)(2,1)} async-done(((bf16[64,4608]{1,0:T(8,128)(2,1)}), bf16[64,4608]{1,0:T(8,128)(2,1)}) %all-reduce.5.cloned.1.call-update) | async-done | bytes 589840 | tf_op jit(solution)/shard_map/psum | solution.py:49
  280.6 2.0 fusion.18
  (14 shorter events, 0.1 us)
Async XLA Ops:
  6.5 32.8 %copy-start = (bf16[256,4608]{1,0:T(8,128)(2,1)S(1)}, bf16[256,4608]{1,0:T(8,128)(2,1)}, u32[]{:S(2)}) copy-start(bf16[256,4608]{1,0:T(8,128)(2,1)} %param.15) | copy-start | bytes 7077892
  6.6 142.2 %all-reduce.3.cloned.1.call-start = ((), (), s32[]{:S(2)}) async-start(), calls=%async_computation | async-start | bytes 1179648 | tf_op jit(solution)/shard_map/psum | solution.py:49
  39.3 1.7 copy-start.3
  39.3 109.4 %copy-start.2 = (bf16[64,4608]{1,0:T(8,128)(2,1)S(1)}, bf16[64,4608]{1,0:T(8,128)(2,1)}, u32[]{:S(2)}) copy-start(bf16[64,4608]{1,0:T(8,128)(2,1)} %param.10) | copy-start | bytes 1769476
  40.7 239.8 %all-reduce.5.cloned.1.call-start = ((), (), s32[]{:S(2)}) async-start(), calls=%async_computation.1 | async-start | bytes 1179648 | tf_op jit(solution)/shard_map/psum | solution.py:49
  150.1 20.7 %slice-start = ((s8[21233664]{0:T(1024)(128)(4,1)}), s8[4194304]{0:T(1024)(128)(4,1)S(1)}, s32[]{:S(2)}) async-start(s8[21233664]{0:T(1024)(128)(4,1)} %bitcast.22), calls=%async_computation.2 | async-start | bytes 8388608
  150.1 20.7 %slice-start.1 = ((s8[21233664]{0:T(1024)(128)(4,1)}), s8[4194304]{0:T(1024)(128)(4,1)S(1)}, s32[]{:S(2)}) async-start(s8[21233664]{0:T(1024)(128)(4,1)} %bitcast.22), calls=%async_computation.3 | async-start | bytes 8388608
  150.1 20.7 %slice-start.2 = ((s8[21233664]{0:T(1024)(128)(4,1)}), s8[4194304]{0:T(1024)(128)(4,1)S(1)}, s32[]{:S(2)}) async-start(s8[21233664]{0:T(1024)(128)(4,1)} %bitcast.22), calls=%async_computation.4 | async-start | bytes 8388608
  159.4 11.4 %slice-start.3 = ((s8[21233664]{0:T(1024)(128)(4,1)}), s8[4194304]{0:T(1024)(128)(4,1)S(1)}, s32[]{:S(2)}) async-start(s8[21233664]{0:T(1024)(128)(4,1)} %bitcast.22), calls=%async_computation.5 | async-start | bytes 8388608
  159.4 11.4 %slice-start.4 = ((s8[21233664]{0:T(1024)(128)(4,1)}), s8[4194304]{0:T(1024)(128)(4,1)S(1)}, s32[]{:S(2)}) async-start(s8[21233664]{0:T(1024)(128)(4,1)} %bitcast.22), calls=%async_computation.6 | async-start | bytes 8388608
  159.4 11.4 %slice-start.5 = ((s8[21233664]{0:T(1024)(128)(4,1)}), s8[262144]{0:T(1024)(128)(4,1)S(1)}, s32[]{:S(2)}) async-start(s8[21233664]{0:T(1024)(128)(4,1)} %bitcast.22), calls=%async_computation.7 | async-start | bytes 524288
  170.8 111.7 %copy-start.1 = (bf16[256,4608]{1,0:T(8,128)(2,1)S(1)}, bf16[256,4608]{1,0:T(8,128)(2,1)}, u32[]{:S(2)}) copy-start(bf16[256,4608]{1,0:T(8,128)(2,1)} %param.15) | copy-start | bytes 7077892
Sparse Core Ops, SparseCore 0:
  40.8 107.8 all-reduce.2
  175.6 104.8 all-reduce.4
where the time goes:
time: 290 us; the launch traced here: 289 us
  waiting for transfers between devices  213 us (73%)
  matrix products  56.8 us (20%)
  between operations  13.6 us (5%)
  other arithmetic  5.71 us (2%)
    psum x2, waiting for transfers between devices, added(): lax.psum(term.astype(jnp.bfloat16), 'tp').astype(jnp.float32)  213 us
    sub x1, matrix products, seen_by(): weights = jax.nn.softmax(scores, -1).astype(jnp.bfloat16)  14.8 us
    dot_general x1, matrix products, einsum(): return jnp.einsum(form, a.astype(jnp.float32), b.astype(jnp.float32))  13 us
    dot_general x1, matrix products, hidden_of(): up = jnp.dot(b, w_up, preferred_element_type=jnp.float32)  11.4 us
    dot_general x1, matrix products, hidden_of(): gate = jnp.dot(b, w_gate, preferred_element_type=jnp.float32)  9.22 us
  transfers between devices with their start and end apart: 2, of which 2 were waited for; matrix products, arithmetic and copies ran while one was open for 0% of the time, Pallas kernels for 0%

commit v1 on v0

v1 whole, which is shorter than its diff:
```python
import functools

import jax
import jax.numpy as jnp
import numpy as np
from jax import lax
from jax.experimental import pallas as pl
from jax.experimental.pallas import tpu as pltpu
from jax.sharding import PartitionSpec as P

HEAD = 128
THETA = 10000
CHUNK = 256
RING = 40
BLOCK = 8
CORES = 2
F32, BF16 = jnp.float32, jnp.bfloat16
MESH = pl.DeviceIdType.MESH


def turns(place):
    half = HEAD // 2
    angle = np.float64(place) * np.float64(THETA) ** (-np.arange(half) / half)
    cos, sin = np.cos(angle), np.sin(angle)
    return np.stack([np.concatenate([cos, cos]), np.concatenate([-sin, sin])]).astype(np.float32)


def layer(chips, x, k, v, gains, wq, wo, wg, wu, wd, rot, out, slots, wq_v, wo_v, gains_v, rot_v, xb, hb, bb, qb, hid,
          own1, ds1, dr1, ss1, sr1, own2, ds2, dr2, ss2, sr2, yb,
          ring_sem, misc_sem, d1s, d1r, r1s, r1r, a1s, a1r, f1s, f1r, d2s, d2r, r2s, r2r, a2s, a2r, f2s, f2r, out_sem):
    d = wq.shape[0]
    half = d // CORES
    cache = k.shape[1]
    hidden = wd.shape[0]
    pairs = BLOCK // 2
    per_block = 2 * pairs
    n_kv = chips * per_block
    n_up = hidden // CHUNK
    n_down = half // CHUNK
    gate_rows = d // 2
    first_down = n_kv + 4 * n_up
    total = first_down + 2 * n_down

    me = lax.axis_index("tp")
    z, c = me // CORES, lax.rem(me, CORES)
    other = 1 - c
    offsets = [chips // 2]
    for far in range(chips // 2 - 1, 0, -1):
        offsets += [far, -far]

    def device(chip, core):
        return {"tp": chip * CORES + core}

    def away(off):
        return lax.rem(z + off + chips, chips)

    def slot_of(off):
        return (-off) % chips - 1

    def dest(j):
        far = chips // 2 - (j + 1) // 2
        return lax.rem(z + jnp.where(lax.rem(j, 2) == 1, far, chips - far), chips)

    def remote(src, dst, send, recv, chip, core):
        return pltpu.make_async_remote_copy(src_ref=src, dst_ref=dst, send_sem=send, recv_sem=recv, device_id=device(chip, core), device_id_type=MESH)

    def arrived(ref, sem):
        pltpu.make_async_copy(ref, ref, sem).wait()

    def two_rows(src, row0, rows, col0, s):
        for e in range(2):
            n = rows // 2
            pltpu.make_async_copy(
                src.at[pl.ds(row0 + e * n, n), pl.ds(pl.multiple_of(col0, CHUNK), CHUNK)], slots.at[s, pl.ds(e * n, n), :], ring_sem.at[s, e]
            ).start()

    def issue(i):
        s = lax.rem(i, RING)

        @pl.when(i < n_kv)
        def _():
            w = lax.rem(i, per_block)
            first = dest(i // per_block) * BLOCK + 2 * lax.rem(w, pairs)

            @pl.when(w < pairs)
            def _():
                for e in range(2):
                    pltpu.make_async_copy(k.at[first + e], slots.at[s, pl.ds(0, cache), pl.ds(e * HEAD, HEAD)], ring_sem.at[s, e]).start()

            @pl.when(w >= pairs)
            def _():
                for e in range(2):
                    pltpu.make_async_copy(v.at[first + e], slots.at[s, pl.ds(0, cache), pl.ds(e * HEAD, HEAD)], ring_sem.at[s, e]).start()

        @pl.when((i >= n_kv) & (i < first_down))
        def _():
            m = i - n_kv
            n, r = m // 4, lax.rem(m, 4)
            row0 = lax.rem(r, 2) * gate_rows

            @pl.when(r < 2)
            def _():
                two_rows(wg, row0, gate_rows, n * CHUNK, s)

            @pl.when(r >= 2)
            def _():
                two_rows(wu, row0, gate_rows, n * CHUNK, s)

        @pl.when((i >= first_down) & (i < total))
        def _():
            m = i - first_down
            core = jnp.where(lax.rem(m, 2) == 0, other, c)
            two_rows(wd, 0, hidden, core * half + (m // 2) * CHUNK, s)

    def ready_cache(s):
        for e in range(2):
            pltpu.make_async_copy(k.at[0], slots.at[s, pl.ds(0, cache), pl.ds(e * HEAD, HEAD)], ring_sem.at[s, e]).wait()

    def ready_rows(src, rows, s):
        for e in range(2):
            n = rows // 2
            pltpu.make_async_copy(src.at[pl.ds(e * n, n), pl.ds(0, CHUNK)], slots.at[s, pl.ds(e * n, n), :], ring_sem.at[s, e]).wait()

    def x_copy(a, b):
        return pltpu.make_async_copy(x.at[pl.ds(a * BLOCK, BLOCK), pl.ds(b * half, half)], xb.at[a, b], misc_sem.at[0])

    for a in range(chips):
        for b in range(CORES):
            x_copy(a, b).start()
    small = [
        pltpu.make_async_copy(gains, gains_v, misc_sem.at[1]),
        pltpu.make_async_copy(rot, rot_v, misc_sem.at[2]),
        pltpu.make_async_copy(wq, wq_v, misc_sem.at[3]),
    ]
    for copy in small:
        copy.start()
    lax.fori_loop(0, per_block, lambda i, _: (issue(i), 0)[1], 0)
    wo_copies = [
        pltpu.make_async_copy(wo.at[:, pl.ds(pl.multiple_of(core * half, CHUNK), half)], wo_v.at[e], misc_sem.at[4 + e])
        for e, core in enumerate((other, c))
    ]
    for copy in wo_copies:
        copy.start()
    lax.fori_loop(per_block, RING, lambda i, _: (issue(i), 0)[1], 0)

    barrier = pltpu.get_barrier_semaphore()
    for off in offsets:
        pl.semaphore_signal(barrier, inc=1, device_id=device(away(off), c), device_id_type=MESH)
    pl.semaphore_signal(barrier, inc=1, device_id=device(z, other), device_id_type=MESH)

    def normed(src, which):
        def two_blocks(m, _):
            rows = [[src[2 * m + a, b].astype(F32) for b in range(CORES)] for a in range(2)]
            scaled = []
            for parts in rows:
                mean = sum(jnp.sum(t * t, -1, keepdims=True) for t in parts) / d
                scale = lax.rsqrt(mean + 1e-6)
                scaled.append([t * scale * gains_v[which : which + 1, b * half : (b + 1) * half] for b, t in enumerate(parts)])
            at = pl.ds(pl.multiple_of(m * 2 * BLOCK, 2 * BLOCK), 2 * BLOCK)
            for b in range(CORES):
                bb[b, at, :] = jnp.concatenate([scaled[0][b], scaled[1][b]], 0).astype(BF16)
            return 0

        lax.fori_loop(0, chips // 2, two_blocks, 0)

    for a in range(2):
        small[a].wait()
    arrived(xb, misc_sem.at[0])
    normed(xb, 0)
    small[2].wait()
    q = jnp.dot(bb[0], wq_v[:half], preferred_element_type=F32) + jnp.dot(bb[1], wq_v[half:], preferred_element_type=F32)
    q = q.astype(BF16).astype(F32)
    turned = []
    for h in range(2):
        t = q[:, h * HEAD : (h + 1) * HEAD]
        turned.append(t * rot_v[0:1, :] + pltpu.roll(t, HEAD // 2, 1) * rot_v[1:2, :])
    for a in range(chips):
        rows = slice(a * BLOCK, (a + 1) * BLOCK)
        qb[a] = jnp.concatenate([turned[0][rows], turned[1][rows]], 0).astype(BF16)
    for copy in wo_copies:
        copy.wait()
    pl.semaphore_wait(barrier, len(offsets) + 1)

    row = lax.rem(lax.broadcasted_iota(jnp.int32, (2 * BLOCK, 2 * HEAD), 0), BLOCK)
    side = lax.broadcasted_iota(jnp.int32, (2 * BLOCK, 2 * HEAD), 1) // HEAD

    def d2d1(j):
        return remote(ds1.at[j], dr1.at[j], d1s.at[j], d1r.at[j], z, other)

    def rs1(j):
        t = dest(j)
        return remote(ss1.at[j], sr1.at[lax.rem(z - t + chips, chips) - 1], r1s.at[j], r1r, t, c)

    def pass_on(j):
        d2d1(j).wait_recv()
        ss1[j] = (own1[j] + dr1[j].astype(F32)).astype(BF16)
        rs1(j).start()

    def attend(j, _):
        base = j * per_block
        q16 = qb[dest(j)]
        wide = jnp.concatenate([q16, q16], 1)
        s = None
        for p in range(pairs):
            slot = lax.rem(base + p, RING)
            ready_cache(slot)
            mine = jnp.where(row == 2 * p + side, wide, jnp.zeros_like(wide))
            part = lax.dot_general(mine, slots[slot, :cache, :], (((1,), (1,)), ((), ())), preferred_element_type=F32)
            s = part if s is None else s + part
        s = s * HEAD**-0.5
        e = jnp.exp(s - jnp.max(s, -1, keepdims=True))
        weights = (e / jnp.sum(e, -1, keepdims=True)).astype(BF16)

        @pl.when(j > 0)
        def _():
            pass_on(j - 1)

        o = None
        for p in range(pairs):
            slot = lax.rem(base + pairs + p, RING)
            ready_cache(slot)
            part = jnp.dot(weights, slots[slot, :cache, :], preferred_element_type=F32)
            part = jnp.where(row == 2 * p + side, part, 0.0)
            o = part if o is None else o + part
        o = o[:, :HEAD] + o[:, HEAD:]
        seen = jnp.concatenate([o[:BLOCK], o[BLOCK:]], 1).astype(BF16)
        ds1[j] = jnp.dot(seen, wo_v[0], preferred_element_type=F32).astype(BF16)
        d2d1(j).start()
        own1[j] = jnp.dot(seen, wo_v[1], preferred_element_type=F32)
        lax.fori_loop(0, per_block, lambda i, _: (issue(base + RING + i), 0)[1], 0)
        return 0

    lax.fori_loop(0, chips, attend, 0)

    d2d1(chips - 1).wait_recv()
    h = own1[chips - 1] + dr1[chips - 1].astype(F32)
    arrived(sr1, r1r)
    for a in range(chips - 1):
        h = h + sr1[a].astype(F32)
    h = h + xb[z, c].astype(F32)
    hb[z, c] = h.astype(BF16)

    def ag1(i):
        off = offsets[i]
        return remote(hb.at[z, c], hb.at[z, c], a1s.at[i], a1r.at[slot_of(off)], away(off), c)

    def fw1(i, chip):
        return remote(hb.at[chip, c], hb.at[chip, c], f1s.at[i], f1r, z, other)

    for i in range(chips - 1):
        ag1(i).start()
    fw1(0, z).start()
    for i in reversed(range(chips - 1)):
        off = offsets[i]
        arrived(hb.at[away(off), c], a1r.at[off % chips - 1])
        fw1(1 + i, away(off)).start()
    arrived(hb.at[:, other], f1r)
    normed(hb, 1)

    def gated(n, _):
        base = n_kv + 4 * n
        parts = []
        for r in range(4):
            slot = lax.rem(base + r, RING)
            ready_rows(wg, gate_rows, slot)
            parts.append(jnp.dot(bb[r % 2], slots[slot, :gate_rows, :], preferred_element_type=F32))
        gate, up = parts[0] + parts[1], parts[2] + parts[3]
        hid[:, pl.ds(pl.multiple_of(n * CHUNK, CHUNK), CHUNK)] = (gate * jax.nn.sigmoid(gate) * up).astype(BF16)
        lax.fori_loop(0, 4, lambda i, _: (issue(base + RING + i), 0)[1], 0)
        return 0

    lax.fori_loop(0, n_up, gated, 0)

    def d2d2(n):
        return remote(ds2.at[n], dr2.at[n], d2s.at[n], d2r.at[n], z, other)

    def rs2(n, i):
        off = offsets[i]
        return remote(ss2.at[n, away(off)], sr2.at[n, slot_of(off)], r2s.at[n, i], r2r.at[n], away(off), c)

    def pass_on2(n):
        d2d2(n).wait_recv()
        t = own2[n] + dr2[n].astype(F32)
        own2[n] = t
        for a in range(chips):
            ss2[n, a] = t[a * BLOCK : (a + 1) * BLOCK].astype(BF16)
        for i in range(chips - 1):
            rs2(n, i).start()

    def down(n, _):
        for e in range(2):
            slot = lax.rem(first_down + 2 * n + e, RING)
            ready_rows(wd, hidden, slot)
            t = jnp.dot(hid[...], slots[slot, :hidden, :], preferred_element_type=F32)
            if e == 0:
                ds2[n] = t.astype(BF16)
                d2d2(n).start()
            else:
                own2[n] = t

        @pl.when(n > 0)
        def _():
            pass_on2(n - 1)

        return 0

    lax.fori_loop(0, n_down, down, 0)
    pass_on2(n_down - 1)

    def ag2(n, i):
        off = offsets[i]
        return remote(yb.at[n, c, z], yb.at[n, c, z], a2s.at[n, i], a2r.at[n], away(off), c)

    def fw2(n):
        return remote(yb.at[n, c], yb.at[n, c], f2s.at[n], f2r.at[n], z, other)

    def finished(n, _):
        arrived(sr2.at[n], r2r.at[n])
        t = own2[n, pl.ds(pl.multiple_of(z * BLOCK, BLOCK), BLOCK), :]
        for a in range(chips - 1):
            t = t + sr2[n, a].astype(F32)
        t = t + hb[z, c, :, pl.ds(pl.multiple_of(n * CHUNK, CHUNK), CHUNK)].astype(F32)
        yb[n, c, z] = t.astype(BF16)
        for i in range(chips - 1):
            ag2(n, i).start()
        return 0

    lax.fori_loop(0, n_down, finished, 0)

    def forward(n, _):
        arrived(yb.at[n, c, pl.ds(0, chips - 1)], a2r.at[n])
        fw2(n).start()
        return 0

    lax.fori_loop(0, n_down, forward, 0)

    def result(n, _):
        arrived(yb.at[n, other], f2r.at[n])
        pltpu.make_async_copy(yb.at[n], out.at[n], out_sem.at[n]).start()
        return 0

    lax.fori_loop(0, n_down, result, 0)

    def sent1(j, _):
        d2d1(j).wait_send()

        @pl.when(j < chips - 1)
        def _():
            rs1(j).wait_send()

        return 0

    lax.fori_loop(0, chips, sent1, 0)
    for i in range(chips - 1):
        ag1(i).wait_send()
        fw1(1 + i, away(offsets[i])).wait_send()
    fw1(0, z).wait_send()

    def sent2(n, _):
        d2d2(n).wait_send()
        for i in range(chips - 1):
            rs2(n, i).wait_send()
            ag2(n, i).wait_send()
        fw2(n).wait_send()
        pltpu.make_async_copy(yb.at[n], out.at[n], out_sem.at[n]).wait()
        return 0

    lax.fori_loop(0, n_down, sent2, 0)


def solution(mesh):
    chips = mesh.shape["tp"] // CORES

    def step(x, k_cache, v_cache, gain_a, wq, wo, gain_m, w_gate, w_up, w_down):
        batch, cache = k_cache.shape[:2]
        d, hidden = x.shape[1], w_down.shape[0]
        half = d // CORES
        k, v = (t.reshape(batch, cache, HEAD) for t in (k_cache, v_cache))
        gains = jnp.stack([gain_a, gain_m]).astype(F32)
        rot = jnp.asarray(turns(cache - 1))
        rows, n_down, peers = max(half, cache, hidden), half // CHUNK, chips - 1
        vmem, dma = pltpu.VMEM, pltpu.SemaphoreType.DMA
        y = pl.pallas_call(
            functools.partial(layer, chips),
            out_shape=jax.ShapeDtypeStruct((n_down, CORES, chips, BLOCK, CHUNK), BF16),
            in_specs=[pl.BlockSpec(memory_space=pl.ANY)] * 10,
            out_specs=pl.BlockSpec(memory_space=pl.ANY),
            scratch_shapes=[
                vmem((RING, rows, CHUNK), BF16),
                vmem(wq.shape, BF16),
                vmem((2, wo.shape[0], half), BF16),
                vmem((2, d), F32),
                vmem((2, HEAD), F32),
                vmem((chips, CORES, BLOCK, half), BF16),
                vmem((chips, CORES, BLOCK, half), BF16),
                vmem((CORES, batch, half), BF16),
                vmem((chips, 2 * BLOCK, HEAD), BF16),
                vmem((batch, hidden), BF16),
                vmem((chips, BLOCK, half), F32),
                vmem((chips, BLOCK, half), BF16),
                vmem((chips, BLOCK, half), BF16),
                vmem((chips, BLOCK, half), BF16),
                vmem((peers, BLOCK, half), BF16),
                vmem((n_down, batch, CHUNK), F32),
                vmem((n_down, batch, CHUNK), BF16),
                vmem((n_down, batch, CHUNK), BF16),
                vmem((n_down, chips, BLOCK, CHUNK), BF16),
                vmem((n_down, peers, BLOCK, CHUNK), BF16),
                vmem((n_down, CORES, chips, BLOCK, CHUNK), BF16),
                dma((RING, 2)),
                dma((6,)),
                dma((chips,)), dma((chips,)), dma((chips,)), dma, dma((peers,)), dma((peers,)), dma((chips,)), dma,
                dma((n_down,)), dma((n_down,)), dma((n_down, peers)), dma((n_down,)), dma((n_down, peers)), dma((n_down,)),
                dma((n_down,)), dma((n_down,)), dma((n_down,)),
            ],
            compiler_params=pltpu.CompilerParams(collective_id=0, has_side_effects=True, vmem_limit_bytes=67_000_000),
            name="decoder_layer",
        )(x, k, v, gains, wq, wo, w_gate, w_up, w_down, rot)
        return y.transpose(2, 3, 1, 0, 4).reshape(batch, d)

    states, cache, columns, rows_of = P("dp", None), P("dp", None, "tp", None), P(None, "tp"), P("tp", None)
    return jax.shard_map(
        step,
        mesh=mesh,
        in_specs=(states, cache, cache, P(None), columns, rows_of, P(None), columns, columns, rows_of),
        out_specs=states,
        check_vma=False,
    )
```

time: 290 us -> 99.4 us (0.34)
  waiting for transfers between devices: 213 us -> 0 us
  Pallas kernels: 0 us -> 95.2 us
  matrix products: 56.8 us -> 0 us
  between operations: 13.6 us -> 0.02 us
  other arithmetic: 5.71 us -> 0.66 us
  local copies, waits for them, and re-layouts: 0.19 us -> 3.35 us
    psum x2 -> x0, waiting for transfers between devices: 213 us -> none  [added(): lax.psum(term.astype(jnp.bfloat16), 'tp').astype(jnp.float32)]
    pallas_call x0 -> x1, Pallas kernels: none -> 95.2 us  [step(): pl.pallas_call(functools.partial(layer, chips), out_shape=jax.ShapeDtypeS...]
    dot_general x6 -> x0, matrix products: 41.9 us -> none  [the longest x1 13 us: einsum(): return jnp.einsum(form, a.astype(jnp.float32), b.astype(jnp.float32))]
    sub x1 -> x0, matrix products: 14.8 us -> none  [seen_by(): weights = jax.nn.softmax(scores, -1).astype(jnp.bfloat16)]
  transfers between devices with their start and end apart: 2 -> 0, of which waited for: 2 -> 0; matrix products, arithmetic and copies ran while one was open for 0% -> 0% of each run, Pallas kernels for 0% -> 0%
where the time goes in v1:
time: 99.4 us; the launch traced here: 99.2 us
  Pallas kernels  95.2 us (96%)
  local copies, waits for them, and re-layouts  3.35 us (3%)
    pallas_call x1, Pallas kernels, step(): pl.pallas_call(functools.partial(layer, chips), out_shape=jax.ShapeDtypeS...  95.2 us

profile of v1, /device:TPU:21, one launch (start us, length us, event | category | flops | bytes accessed | tf_op | source)
XLA Modules:
  0.0 99.2 jit_solution(12941730967146657850)
XLA Ops:
  0.0 0.7 stack.9
  0.7 0.7 stack.10
  1.4 0.7 maximum_convert_fusion.gains
  2.1 95.2 %decoder_layer.1 = bf16[9,2,8,8,256]{4,3,2,1,0:T(8,128)(2,1)} custom-call(bf16[64,4608]{1,0:T(8,128)(2,1)} %x.1, bf16[64,2048,128]{2,1,0:T(8,128)(2,1)} %bitcast.4, bf16[64,2048,128]{2,1,0:T(8,128)(2,1)} %bitcast.5, f32[2,4608]{1,0:T(2,128)} %maximum_convert_fusion.gains, bf16[4608,256]{1,0:T(8,128)(2,1)} %wq.1, bf16[256,4608]{1,0:T(8,128)(2,1)} %wo.1, ...), custom_call_target="tpu_custom_call" | custom-call | tf_op jit(solution)/shard_map/decoder_layer/pallas_call | solution.py:383
  97.3 1.9 %copy.12 = bf16[8,8,2,9,256]{4,1,3,2,0:T(8,128)(2,1)} copy(bf16[8,8,2,9,256]{4,1,0,2,3:T(8,128)(2,1)} %bitcast.6) | data formatting | bytes 1179648 | tf_op jit(solution)/shard_map/transpose | solution.py:419

commit v2 on v1

--- a/solution.py
+++ b/solution.py
@@ -25,7 +25,7 @@
     return np.stack([np.concatenate([cos, cos]), np.concatenate([-sin, sin])]).astype(np.float32)
 
 
-def layer(chips, x, k, v, gains, wq, wo, wg, wu, wd, rot, out, slots, wq_v, wo_v, gains_v, rot_v, xb, hb, bb, qb, hid,
+def layer(chips, x, k, v, gain_a, gain_m, wq, wo, wg, wu, wd, rot, out, slots, wq_v, wo_v, gain_a_v, gain_m_v, rot_v, xb, hb, bb, qb, hid,
           own1, ds1, dr1, ss1, sr1, own2, ds2, dr2, ss2, sr2, yb,
           ring_sem, misc_sem, d1s, d1r, r1s, r1r, a1s, a1r, f1s, f1r, d2s, d2r, r2s, r2r, a2s, a2r, f2s, f2r, out_sem):
     d = wq.shape[0]
@@ -37,9 +37,7 @@
     n_kv = chips * per_block
     n_up = hidden // CHUNK
     n_down = half // CHUNK
-    gate_rows = d // 2
     first_down = n_kv + 4 * n_up
-    total = first_down + 2 * n_down
 
     me = lax.axis_index("tp")
     z, c = me // CORES, lax.rem(me, CORES)
@@ -67,59 +65,46 @@
     def arrived(ref, sem):
         pltpu.make_async_copy(ref, ref, sem).wait()
 
-    def two_rows(src, row0, rows, col0, s):
+    blocks = RING // per_block
+
+    def slot(first, i):
+        at = first % RING + i
+        return jnp.where(at >= RING, at - RING, at)
+
+    def fill_cache(j, s):
+        row0 = dest(j) * BLOCK
+        for w in range(per_block):
+            src = k if w < pairs else v
+            for e in range(2):
+                pltpu.make_async_copy(
+                    src.at[row0 + 2 * (w % pairs) + e], slots.at[s + w, pl.ds(0, cache), pl.ds(e * HEAD, HEAD)], ring_sem.at[s + w]
+                ).start()
+
+    def fill_up(n, s):
+        columns = pl.ds(pl.multiple_of(n * CHUNK, CHUNK), CHUNK)
+        for r in range(4):
+            src = wg if r < 2 else wu
+            pltpu.make_async_copy(src.at[pl.ds(r % 2 * half, half), columns], slots.at[s + r, pl.ds(0, half), :], ring_sem.at[s + r]).start()
+
+    def fill_down(n, s):
+        for e, core in enumerate((other, c)):
+            columns = pl.ds(pl.multiple_of(core * half + n * CHUNK, CHUNK), CHUNK)
+            pltpu.make_async_copy(wd.at[:, columns], slots.at[s + e, pl.ds(0, hidden), :], ring_sem.at[s + e]).start()
+
+    def fill_weights(n, s):
+        @pl.when(n < n_up)
+        def _():
+            fill_up(n, s)
+
         for e in range(2):
-            n = rows // 2
-            pltpu.make_async_copy(
-                src.at[pl.ds(row0 + e * n, n), pl.ds(pl.multiple_of(col0, CHUNK), CHUNK)], slots.at[s, pl.ds(e * n, n), :], ring_sem.at[s, e]
-            ).start()
-
-    def issue(i):
-        s = lax.rem(i, RING)
-
-        @pl.when(i < n_kv)
-        def _():
-            w = lax.rem(i, per_block)
-            first = dest(i // per_block) * BLOCK + 2 * lax.rem(w, pairs)
-
-            @pl.when(w < pairs)
+            m = 2 * (n - n_up) + e
+
+            @pl.when((m >= 0) & (m < n_down))
             def _():
-                for e in range(2):
-                    pltpu.make_async_copy(k.at[first + e], slots.at[s, pl.ds(0, cache), pl.ds(e * HEAD, HEAD)], ring_sem.at[s, e]).start()
-
-            @pl.when(w >= pairs)
-            def _():
-                for e in range(2):
-                    pltpu.make_async_copy(v.at[first + e], slots.at[s, pl.ds(0, cache), pl.ds(e * HEAD, HEAD)], ring_sem.at[s, e]).start()
-
-        @pl.when((i >= n_kv) & (i < first_down))
-        def _():
-            m = i - n_kv
-            n, r = m // 4, lax.rem(m, 4)
-            row0 = lax.rem(r, 2) * gate_rows
-
-            @pl.when(r < 2)
-            def _():
-                two_rows(wg, row0, gate_rows, n * CHUNK, s)
-
-            @pl.when(r >= 2)
-            def _():
-                two_rows(wu, row0, gate_rows, n * CHUNK, s)
-
-        @pl.when((i >= first_down) & (i < total))
-        def _():
-            m = i - first_down
-            core = jnp.where(lax.rem(m, 2) == 0, other, c)
-            two_rows(wd, 0, hidden, core * half + (m // 2) * CHUNK, s)
-
-    def ready_cache(s):
-        for e in range(2):
-            pltpu.make_async_copy(k.at[0], slots.at[s, pl.ds(0, cache), pl.ds(e * HEAD, HEAD)], ring_sem.at[s, e]).wait()
-
-    def ready_rows(src, rows, s):
-        for e in range(2):
-            n = rows // 2
-            pltpu.make_async_copy(src.at[pl.ds(e * n, n), pl.ds(0, CHUNK)], slots.at[s, pl.ds(e * n, n), :], ring_sem.at[s, e]).wait()
+                fill_down(m, s + 2 * e)
+
+    def ready(s, rows):
+        arrived(slots.at[s, pl.ds(0, rows), :], ring_sem.at[s])
 
     def x_copy(a, b):
         return pltpu.make_async_copy(x.at[pl.ds(a * BLOCK, BLOCK), pl.ds(b * half, half)], xb.at[a, b], misc_sem.at[0])
@@ -127,21 +112,9 @@
     for a in range(chips):
         for b in range(CORES):
             x_copy(a, b).start()
-    small = [
-        pltpu.make_async_copy(gains, gains_v, misc_sem.at[1]),
-        pltpu.make_async_copy(rot, rot_v, misc_sem.at[2]),
-        pltpu.make_async_copy(wq, wq_v, misc_sem.at[3]),
-    ]
+    small = [pltpu.make_async_copy(src, dst, misc_sem.at[1 + i]) for i, (src, dst) in enumerate(((gain_a, gain_a_v), (gain_m, gain_m_v), (rot, rot_v), (wq, wq_v)))]
     for copy in small:
         copy.start()
-    lax.fori_loop(0, per_block, lambda i, _: (issue(i), 0)[1], 0)
-    wo_copies = [
-        pltpu.make_async_copy(wo.at[:, pl.ds(pl.multiple_of(core * half, CHUNK), half)], wo_v.at[e], misc_sem.at[4 + e])
-        for e, core in enumerate((other, c))
-    ]
-    for copy in wo_copies:
-        copy.start()
-    lax.fori_loop(per_block, RING, lambda i, _: (issue(i), 0)[1], 0)
 
     barrier = pltpu.get_barrier_semaphore()
     for off in offsets:
@@ -149,13 +122,15 @@
     pl.semaphore_signal(barrier, inc=1, device_id=device(z, other), device_id_type=MESH)
 
     def normed(src, which):
+        gain = which[...].astype(F32).reshape(1, d)
+
         def two_blocks(m, _):
             rows = [[src[2 * m + a, b].astype(F32) for b in range(CORES)] for a in range(2)]
             scaled = []
             for parts in rows:
                 mean = sum(jnp.sum(t * t, -1, keepdims=True) for t in parts) / d
                 scale = lax.rsqrt(mean + 1e-6)
-                scaled.append([t * scale * gains_v[which : which + 1, b * half : (b + 1) * half] for b, t in enumerate(parts)])
+                scaled.append([t * scale * gain[:, b * half : (b + 1) * half] for b, t in enumerate(parts)])
             at = pl.ds(pl.multiple_of(m * 2 * BLOCK, 2 * BLOCK), 2 * BLOCK)
             for b in range(CORES):
                 bb[b, at, :] = jnp.concatenate([scaled[0][b], scaled[1][b]], 0).astype(BF16)
@@ -163,11 +138,24 @@
 
         lax.fori_loop(0, chips // 2, two_blocks, 0)
 
-    for a in range(2):
+    arrived(xb, misc_sem.at[0])
+
+    def fill_first(j, _):
+        fill_cache(j, j * per_block)
+        return 0
+
+    lax.fori_loop(0, 1, fill_first, 0)
+    wo_copies = [
+        pltpu.make_async_copy(wo.at[:, pl.ds(pl.multiple_of(core * half, CHUNK), half)], wo_v.at[e], misc_sem.at[5 + e])
+        for e, core in enumerate((other, c))
+    ]
+    for copy in wo_copies:
+        copy.start()
+    lax.fori_loop(1, blocks, fill_first, 0)
+    for a in range(3):
         small[a].wait()
-    arrived(xb, misc_sem.at[0])
-    normed(xb, 0)
-    small[2].wait()
+    normed(xb, gain_a_v)
+    small[3].wait()
     q = jnp.dot(bb[0], wq_v[:half], preferred_element_type=F32) + jnp.dot(bb[1], wq_v[half:], preferred_element_type=F32)
     q = q.astype(BF16).astype(F32)
     turned = []
@@ -179,7 +167,6 @@
         qb[a] = jnp.concatenate([turned[0][rows], turned[1][rows]], 0).astype(BF16)
     for copy in wo_copies:
         copy.wait()
-    pl.semaphore_wait(barrier, len(offsets) + 1)
 
     row = lax.rem(lax.broadcasted_iota(jnp.int32, (2 * BLOCK, 2 * HEAD), 0), BLOCK)
     side = lax.broadcasted_iota(jnp.int32, (2 * BLOCK, 2 * HEAD), 1) // HEAD
@@ -197,29 +184,33 @@
         rs1(j).start()
 
     def attend(j, _):
-        base = j * per_block
+        base = slot(0, j * per_block)
         q16 = qb[dest(j)]
         wide = jnp.concatenate([q16, q16], 1)
+        for p in range(pairs):
+            ready(base + p, cache)
         s = None
         for p in range(pairs):
-            slot = lax.rem(base + p, RING)
-            ready_cache(slot)
             mine = jnp.where(row == 2 * p + side, wide, jnp.zeros_like(wide))
-            part = lax.dot_general(mine, slots[slot, :cache, :], (((1,), (1,)), ((), ())), preferred_element_type=F32)
+            part = lax.dot_general(mine, slots[base + p, :cache, :], (((1,), (1,)), ((), ())), preferred_element_type=F32)
             s = part if s is None else s + part
         s = s * HEAD**-0.5
         e = jnp.exp(s - jnp.max(s, -1, keepdims=True))
         weights = (e / jnp.sum(e, -1, keepdims=True)).astype(BF16)
 
+        @pl.when(j == 0)
+        def _():
+            pl.semaphore_wait(barrier, len(offsets) + 1)
+
         @pl.when(j > 0)
         def _():
             pass_on(j - 1)
 
+        for p in range(pairs):
+            ready(base + pairs + p, cache)
         o = None
         for p in range(pairs):
-            slot = lax.rem(base + pairs + p, RING)
-            ready_cache(slot)
-            part = jnp.dot(weights, slots[slot, :cache, :], preferred_element_type=F32)
+            part = jnp.dot(weights, slots[base + pairs + p, :cache, :], preferred_element_type=F32)
             part = jnp.where(row == 2 * p + side, part, 0.0)
             o = part if o is None else o + part
         o = o[:, :HEAD] + o[:, HEAD:]
@@ -227,7 +218,16 @@
         ds1[j] = jnp.dot(seen, wo_v[0], preferred_element_type=F32).astype(BF16)
         d2d1(j).start()
         own1[j] = jnp.dot(seen, wo_v[1], preferred_element_type=F32)
-        lax.fori_loop(0, per_block, lambda i, _: (issue(base + RING + i), 0)[1], 0)
+
+        @pl.when(j < chips - blocks)
+        def _():
+            fill_cache(j + blocks, base)
+
+        @pl.when(j >= chips - blocks)
+        def _():
+            for e in range(2):
+                fill_weights(2 * (j - (chips - blocks)) + e, base + 4 * e)
+
         return 0
 
     lax.fori_loop(0, chips, attend, 0)
@@ -255,18 +255,16 @@
         arrived(hb.at[away(off), c], a1r.at[off % chips - 1])
         fw1(1 + i, away(off)).start()
     arrived(hb.at[:, other], f1r)
-    normed(hb, 1)
+    normed(hb, gain_m_v)
 
     def gated(n, _):
-        base = n_kv + 4 * n
-        parts = []
+        base = slot(n_kv, 4 * n)
         for r in range(4):
-            slot = lax.rem(base + r, RING)
-            ready_rows(wg, gate_rows, slot)
-            parts.append(jnp.dot(bb[r % 2], slots[slot, :gate_rows, :], preferred_element_type=F32))
+            ready(base + r, half)
+        parts = [jnp.dot(bb[r % 2], slots[base + r, :half, :], preferred_element_type=F32) for r in range(4)]
         gate, up = parts[0] + parts[1], parts[2] + parts[3]
         hid[:, pl.ds(pl.multiple_of(n * CHUNK, CHUNK), CHUNK)] = (gate * jax.nn.sigmoid(gate) * up).astype(BF16)
-        lax.fori_loop(0, 4, lambda i, _: (issue(base + RING + i), 0)[1], 0)
+        fill_weights(n + 2 * blocks, base)
         return 0
 
     lax.fori_loop(0, n_up, gated, 0)
@@ -289,9 +287,9 @@
 
     def down(n, _):
         for e in range(2):
-            slot = lax.rem(first_down + 2 * n + e, RING)
-            ready_rows(wd, hidden, slot)
-            t = jnp.dot(hid[...], slots[slot, :hidden, :], preferred_element_type=F32)
+            at = slot(first_down, 2 * n) + e
+            ready(at, hidden)
+            t = jnp.dot(hid[...], slots[at, :hidden, :], preferred_element_type=F32)
             if e == 0:
                 ds2[n] = t.astype(BF16)
                 d2d2(n).start()
@@ -376,20 +374,20 @@
         d, hidden = x.shape[1], w_down.shape[0]
         half = d // CORES
         k, v = (t.reshape(batch, cache, HEAD) for t in (k_cache, v_cache))
-        gains = jnp.stack([gain_a, gain_m]).astype(F32)
         rot = jnp.asarray(turns(cache - 1))
         rows, n_down, peers = max(half, cache, hidden), half // CHUNK, chips - 1
         vmem, dma = pltpu.VMEM, pltpu.SemaphoreType.DMA
         y = pl.pallas_call(
             functools.partial(layer, chips),
             out_shape=jax.ShapeDtypeStruct((n_down, CORES, chips, BLOCK, CHUNK), BF16),
-            in_specs=[pl.BlockSpec(memory_space=pl.ANY)] * 10,
+            in_specs=[pl.BlockSpec(memory_space=pl.ANY)] * 11,
             out_specs=pl.BlockSpec(memory_space=pl.ANY),
             scratch_shapes=[
                 vmem((RING, rows, CHUNK), BF16),
                 vmem(wq.shape, BF16),
                 vmem((2, wo.shape[0], half), BF16),
-                vmem((2, d), F32),
+                vmem((d,), BF16),
+                vmem((d,), BF16),
                 vmem((2, HEAD), F32),
                 vmem((chips, CORES, BLOCK, half), BF16),
                 vmem((chips, CORES, BLOCK, half), BF16),
@@ -407,15 +405,15 @@
                 vmem((n_down, chips, BLOCK, CHUNK), BF16),
                 vmem((n_down, peers, BLOCK, CHUNK), BF16),
                 vmem((n_down, CORES, chips, BLOCK, CHUNK), BF16),
-                dma((RING, 2)),
-                dma((6,)),
+                dma((RING,)),
+                dma((7,)),
                 dma((chips,)), dma((chips,)), dma((chips,)), dma, dma((peers,)), dma((peers,)), dma((chips,)), dma,
                 dma((n_down,)), dma((n_down,)), dma((n_down, peers)), dma((n_down,)), dma((n_down, peers)), dma((n_down,)),
                 dma((n_down,)), dma((n_down,)), dma((n_down,)),
             ],
             compiler_params=pltpu.CompilerParams(collective_id=0, has_side_effects=True, vmem_limit_bytes=67_000_000),
             name="decoder_layer",
-        )(x, k, v, gains, wq, wo, w_gate, w_up, w_down, rot)
+        )(x, k, v, gain_a, gain_m, wq, wo, w_gate, w_up, w_down, rot)
         return y.transpose(2, 3, 1, 0, 4).reshape(batch, d)
 
     states, cache, columns, rows_of = P("dp", None), P("dp", None, "tp", None), P(None, "tp"), P("tp", None)

time: 99.4 us -> 79.9 us (0.80)
  Pallas kernels: 95.2 us -> 77.8 us
  local copies, waits for them, and re-layouts: 3.35 us -> 1.92 us
    pallas_call x1, Pallas kernels: 95.2 us -> 77.8 us  [step(): pl.pallas_call(functools.partial(layer, chips), out_shape=jax.ShapeDtypeS...]
    another operation x2 -> x0, local copies, waits for them, and re-layouts: 1.43 us -> none  [step(): gains = jnp.stack([gain_a, gain_m]).astype(F32)]
where the time goes in v2:
time: 79.9 us; the launch traced here: 79.7 us
  Pallas kernels  77.8 us (97%)
  local copies, waits for them, and re-layouts  1.92 us (2%)
    pallas_call x1, Pallas kernels, step(): pl.pallas_call(functools.partial(layer, chips), out_shape=jax.ShapeDtypeS...  77.8 us
    transpose x1, local copies, waits for them, and re-layouts, step(): return y.transpose(2, 3, 1, 0, 4).reshape(batch, d)  1.92 us

profile of v2, /device:TPU:21, one launch (start us, length us, event | category | flops | bytes accessed | tf_op | source)
XLA Modules:
  0.0 79.7 jit_solution(12348271086937470762)
XLA Ops:
  0.0 77.8 %decoder_layer.1 = bf16[9,2,8,8,256]{4,3,2,1,0:T(8,128)(2,1)} custom-call(bf16[64,4608]{1,0:T(8,128)(2,1)} %x.1, bf16[64,2048,128]{2,1,0:T(8,128)(2,1)} %bitcast.4, bf16[64,2048,128]{2,1,0:T(8,128)(2,1)} %bitcast.5, bf16[4608]{0:T(1024)(128)(2,1)} %gain_a.1, bf16[4608]{0:T(1024)(128)(2,1)} %gain_m.1, bf16[4608,256]{1,0:T(8,128)(2,1)} %wq.1, ...), custom_call_target="tpu_custom_call" | custom-call | tf_op jit(solution)/shard_map/decoder_layer/pallas_call | solution.py:380
  77.8 1.9 %copy.12 = bf16[8,8,2,9,256]{4,1,3,2,0:T(8,128)(2,1)} copy(bf16[8,8,2,9,256]{4,1,0,2,3:T(8,128)(2,1)} %bitcast.6) | data formatting | bytes 1179648 | tf_op jit(solution)/shard_map/transpose | solution.py:417

commit v3 on v2

--- a/solution.py
+++ b/solution.py
@@ -116,6 +116,19 @@
     for copy in small:
         copy.start()
 
+    def fill_first(j, _):
+        fill_cache(j, j * per_block)
+        return 0
+
+    lax.fori_loop(0, 1, fill_first, 0)
+    wo_copies = [
+        pltpu.make_async_copy(wo.at[:, pl.ds(pl.multiple_of(core * half, CHUNK), half)], wo_v.at[e], misc_sem.at[5 + e])
+        for e, core in enumerate((other, c))
+    ]
+    for copy in wo_copies:
+        copy.start()
+    lax.fori_loop(1, blocks, fill_first, 0)
+
     barrier = pltpu.get_barrier_semaphore()
     for off in offsets:
         pl.semaphore_signal(barrier, inc=1, device_id=device(away(off), c), device_id_type=MESH)
@@ -139,19 +152,6 @@
         lax.fori_loop(0, chips // 2, two_blocks, 0)
 
     arrived(xb, misc_sem.at[0])
-
-    def fill_first(j, _):
-        fill_cache(j, j * per_block)
-        return 0
-
-    lax.fori_loop(0, 1, fill_first, 0)
-    wo_copies = [
-        pltpu.make_async_copy(wo.at[:, pl.ds(pl.multiple_of(core * half, CHUNK), half)], wo_v.at[e], misc_sem.at[5 + e])
-        for e, core in enumerate((other, c))
-    ]
-    for copy in wo_copies:
-        copy.start()
-    lax.fori_loop(1, blocks, fill_first, 0)
     for a in range(3):
         small[a].wait()
     normed(xb, gain_a_v)
@@ -172,11 +172,11 @@
     side = lax.broadcasted_iota(jnp.int32, (2 * BLOCK, 2 * HEAD), 1) // HEAD
 
     def d2d1(j):
-        return remote(ds1.at[j], dr1.at[j], d1s.at[j], d1r.at[j], z, other)
+        return remote(ds1.at[j], dr1.at[j], d1s, d1r.at[j], z, other)
 
     def rs1(j):
         t = dest(j)
-        return remote(ss1.at[j], sr1.at[lax.rem(z - t + chips, chips) - 1], r1s.at[j], r1r, t, c)
+        return remote(ss1.at[j], sr1.at[lax.rem(z - t + chips, chips) - 1], r1s, r1r, t, c)
 
     def pass_on(j):
         d2d1(j).wait_recv()
@@ -242,18 +242,18 @@
 
     def ag1(i):
         off = offsets[i]
-        return remote(hb.at[z, c], hb.at[z, c], a1s.at[i], a1r.at[slot_of(off)], away(off), c)
-
-    def fw1(i, chip):
-        return remote(hb.at[chip, c], hb.at[chip, c], f1s.at[i], f1r, z, other)
+        return remote(hb.at[z, c], hb.at[z, c], a1s, a1r.at[slot_of(off)], away(off), c)
+
+    def fw1(chip):
+        return remote(hb.at[chip, c], hb.at[chip, c], f1s, f1r, z, other)
 
     for i in range(chips - 1):
         ag1(i).start()
-    fw1(0, z).start()
+    fw1(z).start()
     for i in reversed(range(chips - 1)):
         off = offsets[i]
         arrived(hb.at[away(off), c], a1r.at[off % chips - 1])
-        fw1(1 + i, away(off)).start()
+        fw1(away(off)).start()
     arrived(hb.at[:, other], f1r)
     normed(hb, gain_m_v)
 
@@ -270,11 +270,11 @@
     lax.fori_loop(0, n_up, gated, 0)
 
     def d2d2(n):
-        return remote(ds2.at[n], dr2.at[n], d2s.at[n], d2r.at[n], z, other)
+        return remote(ds2.at[n], dr2.at[n], d2s, d2r.at[n], z, other)
 
     def rs2(n, i):
         off = offsets[i]
-        return remote(ss2.at[n, away(off)], sr2.at[n, slot_of(off)], r2s.at[n, i], r2r.at[n], away(off), c)
+        return remote(ss2.at[n, away(off)], sr2.at[n, slot_of(off)], r2s, r2r.at[n], away(off), c)
 
     def pass_on2(n):
         d2d2(n).wait_recv()
@@ -284,6 +284,20 @@
             ss2[n, a] = t[a * BLOCK : (a + 1) * BLOCK].astype(BF16)
         for i in range(chips - 1):
             rs2(n, i).start()
+
+    def ag2(n, i):
+        off = offsets[i]
+        return remote(yb.at[n, z], yb.at[n, z], a2s, a2r.at[n], away(off), c)
+
+    def finished(n):
+        arrived(sr2.at[n], r2r.at[n])
+        t = own2[n, pl.ds(pl.multiple_of(z * BLOCK, BLOCK), BLOCK), :]
+        for a in range(chips - 1):
+            t = t + sr2[n, a].astype(F32)
+        t = t + hb[z, c, :, pl.ds(pl.multiple_of(n * CHUNK, CHUNK), CHUNK)].astype(F32)
+        yb[n, z] = t.astype(BF16)
+        for i in range(chips - 1):
+            ag2(n, i).start()
 
     def down(n, _):
         for e in range(2):
@@ -304,66 +318,35 @@
 
     lax.fori_loop(0, n_down, down, 0)
     pass_on2(n_down - 1)
-
-    def ag2(n, i):
-        off = offsets[i]
-        return remote(yb.at[n, c, z], yb.at[n, c, z], a2s.at[n, i], a2r.at[n], away(off), c)
+    lax.fori_loop(0, n_down, lambda n, _: (finished(n), 0)[1], 0)
+
+    def columns_of(core, n):
+        return out.at[:, :, pl.ds(pl.multiple_of(core * half + n * CHUNK, CHUNK), CHUNK)]
+
+    def kept(n):
+        return pltpu.make_async_copy(yb.at[n], columns_of(c, n), out_sem)
 
     def fw2(n):
-        return remote(yb.at[n, c], yb.at[n, c], f2s.at[n], f2r.at[n], z, other)
-
-    def finished(n, _):
-        arrived(sr2.at[n], r2r.at[n])
-        t = own2[n, pl.ds(pl.multiple_of(z * BLOCK, BLOCK), BLOCK), :]
-        for a in range(chips - 1):
-            t = t + sr2[n, a].astype(F32)
-        t = t + hb[z, c, :, pl.ds(pl.multiple_of(n * CHUNK, CHUNK), CHUNK)].astype(F32)
-        yb[n, c, z] = t.astype(BF16)
-        for i in range(chips - 1):
-            ag2(n, i).start()
+        return remote(yb.at[n], columns_of(c, n), f2s, f2r, z, other)
+
+    def forward(n, _):
+        arrived(yb.at[n, pl.ds(0, chips - 1)], a2r.at[n])
+        fw2(n).start()
+        kept(n).start()
         return 0
 
-    lax.fori_loop(0, n_down, finished, 0)
-
-    def forward(n, _):
-        arrived(yb.at[n, c, pl.ds(0, chips - 1)], a2r.at[n])
-        fw2(n).start()
-        return 0
-
     lax.fori_loop(0, n_down, forward, 0)
 
-    def result(n, _):
-        arrived(yb.at[n, other], f2r.at[n])
-        pltpu.make_async_copy(yb.at[n], out.at[n], out_sem.at[n]).start()
-        return 0
-
-    lax.fori_loop(0, n_down, result, 0)
-
-    def sent1(j, _):
-        d2d1(j).wait_send()
-
-        @pl.when(j < chips - 1)
-        def _():
-            rs1(j).wait_send()
-
-        return 0
-
-    lax.fori_loop(0, chips, sent1, 0)
-    for i in range(chips - 1):
-        ag1(i).wait_send()
-        fw1(1 + i, away(offsets[i])).wait_send()
-    fw1(0, z).wait_send()
-
-    def sent2(n, _):
-        d2d2(n).wait_send()
-        for i in range(chips - 1):
-            rs2(n, i).wait_send()
-            ag2(n, i).wait_send()
-        fw2(n).wait_send()
-        pltpu.make_async_copy(yb.at[n], out.at[n], out_sem.at[n]).wait()
-        return 0
-
-    lax.fori_loop(0, n_down, sent2, 0)
+    arrived(ds1, d1s)
+    arrived(sr1, r1s)
+    arrived(sr1, a1s)
+    arrived(ds1, f1s)
+    arrived(ds2, d2s)
+    arrived(sr2, r2s)
+    arrived(sr2, a2s)
+    arrived(yb, f2s)
+    arrived(yb, out_sem)
+    arrived(yb, f2r)
 
 
 def solution(mesh):
@@ -379,7 +362,7 @@
         vmem, dma = pltpu.VMEM, pltpu.SemaphoreType.DMA
         y = pl.pallas_call(
             functools.partial(layer, chips),
-            out_shape=jax.ShapeDtypeStruct((n_down, CORES, chips, BLOCK, CHUNK), BF16),
+            out_shape=jax.ShapeDtypeStruct((chips, BLOCK, d), BF16),
             in_specs=[pl.BlockSpec(memory_space=pl.ANY)] * 11,
             out_specs=pl.BlockSpec(memory_space=pl.ANY),
             scratch_shapes=[
@@ -404,17 +387,16 @@
                 vmem((n_down, batch, CHUNK), BF16),
                 vmem((n_down, chips, BLOCK, CHUNK), BF16),
                 vmem((n_down, peers, BLOCK, CHUNK), BF16),
-                vmem((n_down, CORES, chips, BLOCK, CHUNK), BF16),
+                vmem((n_down, chips, BLOCK, CHUNK), BF16),
                 dma((RING,)),
                 dma((7,)),
-                dma((chips,)), dma((chips,)), dma((chips,)), dma, dma((peers,)), dma((peers,)), dma((chips,)), dma,
-                dma((n_down,)), dma((n_down,)), dma((n_down, peers)), dma((n_down,)), dma((n_down, peers)), dma((n_down,)),
-                dma((n_down,)), dma((n_down,)), dma((n_down,)),
+                dma, dma((chips,)), dma, dma, dma, dma((peers,)), dma, dma,
+                dma, dma((n_down,)), dma, dma((n_down,)), dma, dma((n_down,)), dma, dma, dma,
             ],
             compiler_params=pltpu.CompilerParams(collective_id=0, has_side_effects=True, vmem_limit_bytes=67_000_000),
             name="decoder_layer",
         )(x, k, v, gain_a, gain_m, wq, wo, w_gate, w_up, w_down, rot)
-        return y.transpose(2, 3, 1, 0, 4).reshape(batch, d)
+        return y.reshape(batch, d)
 
     states, cache, columns, rows_of = P("dp", None), P("dp", None, "tp", None), P(None, "tp"), P("tp", None)
     return jax.shard_map(

time: 79.9 us -> 77.4 us (0.969)
  Pallas kernels: 77.8 us -> 75.4 us
    pallas_call x1, Pallas kernels: 77.8 us -> 75.4 us  [step(): pl.pallas_call(functools.partial(layer, chips), out_shape=jax.ShapeDtypeS...]
    transpose x1 -> x0, local copies, waits for them, and re-layouts: 1.92 us -> none  [step(): return y.transpose(2, 3, 1, 0, 4).reshape(batch, d)]
    unnamed x0 -> x1, local copies, waits for them, and re-layouts: none -> 1.92 us
where the time goes in v3:
time: 77.4 us; the launch traced here: 77.3 us
  Pallas kernels  75.4 us (97%)
  local copies, waits for them, and re-layouts  1.92 us (2%)
    pallas_call x1, Pallas kernels, step(): pl.pallas_call(functools.partial(layer, chips), out_shape=jax.ShapeDtypeS...  75.4 us
    unnamed x1, local copies, waits for them, and re-layouts  1.92 us

profile of v3, /device:TPU:21, one launch (start us, length us, event | category | flops | bytes accessed | tf_op | source)
XLA Modules:
  0.0 77.3 jit_solution(14859985290325123997)
XLA Ops:
  0.0 75.4 %decoder_layer.1 = bf16[8,8,4608]{2,1,0:T(8,128)(2,1)} custom-call(bf16[64,4608]{1,0:T(8,128)(2,1)} %x.1, bf16[64,2048,128]{2,1,0:T(8,128)(2,1)} %bitcast.3, bf16[64,2048,128]{2,1,0:T(8,128)(2,1)} %bitcast.4, bf16[4608]{0:T(1024)(128)(2,1)} %gain_a.1, bf16[4608]{0:T(1024)(128)(2,1)} %gain_m.1, bf16[4608,256]{1,0:T(8,128)(2,1)} %wq.1, bf16[256,4608]{1,0:T(8,128)(2,1)} %wo.1, ...), custom_call_target="tpu_custom_call" | custom-call | tf_op jit(solution)/shard_map/decoder_layer/pallas_call | solution.py:363
  75.4 1.9 %copy.13 = bf16[64,4608]{1,0:T(8,128)(2,1)} copy(bf16[64,4608]{1,0:T(8,128)(2,1)} %bitcast.5) | data formatting | bytes 1179648
